TPU v7x, 32 devices: a whole 2x2x4 slice. The times are simulated.
32 devices in a mesh: cluster: 4 (over x, core), leaf: 8 (over z, y).
Axes of the slice: x: 2, y: 2, z: 4, core: 2. Of those that a mesh axis runs over, the one named last changes fastest.
Arguments:
- probes: float32 [32768, 512], P(('cluster', 'leaf')), may hold values from -6 to 6
- dense_leaf: float32 [32768, 1024], P(('cluster', 'leaf')), may hold values from -0.1875 to 0.1875
- leaf_basis: float32 [32768, 128], P(('cluster', 'leaf')), may hold values from -0.1875 to 0.1875
- sibling_cores: float32 [32, 8, 128, 128], P(('cluster', 'leaf')), may hold values from -0.5 to 0.5
- transfer: float32 [32, 128, 128], P(('cluster', 'leaf')), may hold values from -0.5 to 0.5
- cluster_cores: float32 [4, 4, 128, 128], P('cluster'), may hold values from -0.1875 to 0.1875
Outputs:
- product: float32 [32768, 512], P(('cluster', 'leaf'))
All inputs are finite; a program needn't handle non-finite values.
Results may differ from a plain program's by a relative error of at most 0.00005.
Values sent between devices are 32-bit elements; how exact they have to be, the bound alone decides.
No kernel may reach another device: no remote copies, remote signals or barrier semaphores. Data moves between devices by JAX's collectives and lax.ppermute only.
A program may use at most 128 MiB of HBM per device.

v0:
```python
import jax
import jax.numpy as jnp
from jax import lax
from jax.sharding import PartitionSpec as P

HI = lax.Precision.HIGHEST


def local(probes, dense_leaf, leaf_basis, sibling_cores, transfer, cluster_cores):
    own = lax.axis_index("leaf")
    cown = lax.axis_index("cluster")
    cores = sibling_cores[0]
    trans = transfer[0]
    outer_cores = cluster_cores[0]
    rank_two = trans.shape[1]
    near = jnp.dot(dense_leaf, probes, precision=HI) + jnp.dot(dense_leaf.T, probes, precision=HI)
    coef = jnp.dot(leaf_basis.T, probes, precision=HI)
    turned = lax.all_to_all(cores, "leaf", split_axis=0, concat_axis=0, tiled=True)
    used = cores + jnp.transpose(turned, (0, 2, 1))
    piece = lax.all_gather(coef[None], "leaf", axis=0, tiled=True)
    count = piece.shape[0]
    block = used
    keep = (jnp.arange(count, dtype=jnp.int32) != own).astype(jnp.float32)
    block = block * keep[:, None, None]
    sib = jnp.einsum("jab,jbp->ap", block, piece, precision=HI)
    local_g = jnp.dot(trans.T, coef, precision=HI)
    nclu = outer_cores.shape[0]
    bkeep = (jnp.arange(nclu, dtype=jnp.int32) != cown).astype(jnp.float32)[:, None, None]
    masked = outer_cores * bkeep
    g_whole = lax.psum(local_g, "leaf")
    gathered = lax.all_gather(g_whole[None], "cluster", axis=0, tiled=True)
    front = jnp.einsum("dab,dbp->ap", masked, gathered, precision=HI)
    number = rank_two * lax.axis_size("cluster") // rank_two
    block = masked
    terms = jnp.einsum("dba,bp->dap", block, g_whole, precision=HI)
    field = front + lax.psum_scatter(
        terms.reshape(number * rank_two, g_whole.shape[1]),
        "cluster",
        scatter_dimension=0,
        tiled=True,
    )
    total = sib + jnp.dot(trans, field, precision=HI)
    return near + jnp.dot(leaf_basis, total, precision=HI)


def solution(mesh):
    return jax.shard_map(
        local,
        mesh=mesh,
        in_specs=(
            P(("cluster", "leaf"), None),
            P(("cluster", "leaf"), None),
            P(("cluster", "leaf"), None),
            P(("cluster", "leaf"), None, None, None),
            P(("cluster", "leaf"), None, None),
            P("cluster", None, None, None),
        ),
        out_specs=P(("cluster", "leaf"), None),
        check_vma=False,
    )
```

profile of v0, /device:TPU:0, one launch (start us, length us, event | category | flops | bytes accessed | tf_op | source)
XLA Modules:
  0.0 197.5 jit_solution(9313554170039844846)
XLA Ops:
  6.5 1.6 copy-done
  8.1 2.4 %fusion.10 = f32[128,512]{1,0:T(8,128)S(1)} fusion(f32[1024,128]{1,0:T(8,128)} %param.8, f32[1024,512]{1,0:T(8,128)S(1)} %copy-done), kind=kOutput, calls=%fused_computation.18 | convolution fusion | flops 805306368 | bytes 2883584 | tf_op jit(solution)/shard_map/dot_general | solution.py:17
  10.6 1.3 convolution_bitcast_fusion.3
  11.9 0.0 all-reduce.2.cloned.1.call-update
  11.9 0.0 all-gather.7.cloned.1.call-start
  11.9 73.8 %all-reduce.2.cloned.1.call-done = f32[128,512]{0,1:T(8,128)} async-done(((f32[128,512]{0,1:T(8,128)}), f32[128,512]{0,1:T(8,128)}) %all-reduce.2.cloned.1.call-update) | async-done | bytes 262160 | tf_op jit(solution)/shard_map/psum | solution.py:30
  85.8 0.0 reduce-scatter.2.cloned.1.call-start
  85.8 0.1 copy.10
  86.0 0.1 bitcast_multiply_fusion
  86.1 2.9 %fusion.11 = f32[512,512]{1,0:T(8,128)} fusion(f32[512,128]{1,0:T(8,128)S(1)} %bitcast.52, f32[128,512]{0,1:T(8,128)} %all-reduce.2.cloned.1.call-done), kind=kOutput, calls=%fused_computation.19 | convolution fusion | flops 402653184 | bytes 1572864 | tf_op jit(solution)/shard_map/dba,bp->dap/dot_general | solution.py:35
  89.0 0.0 reduce-scatter.2.cloned.1.call-update
  89.1 0.0 all-gather.5.cloned.1.call-start
  89.1 0.5 all-gather.5.cloned.1.call-update
  89.6 1.0 copy.9
  90.6 4.3 %all-to-all-start = ((f32[8,128,128]{1,2,0:T(8,128)}), f32[8,128,128]{1,2,0:T(8,128)}, u32[]{:S(2)}, u32[]{:S(2)}) async-start(f32[8,128,128]{1,2,0:T(8,128)} %copy.9), calls=%async_computation | async-start | bytes 1048576 | tf_op jit(solution)/shard_map/all_to_all | solution.py:18
  95.0 9.6 %fusion.8 = f32[1024,512]{1,0:T(8,128)} fusion(f32[1024,1024]{1,0:T(8,128)} %param.7, f32[1024,512]{1,0:T(8,128)S(1)} %copy-done), kind=kOutput, calls=%fused_computation.16 | convolution fusion | flops 6442450944 | bytes 8388608 | tf_op jit(solution)/shard_map/dot_general | solution.py:16
  104.6 9.6 %fusion.9 = f32[1024,512]{1,0:T(8,128)} fusion(f32[1024,1024]{1,0:T(8,128)} %param.7, f32[1024,512]{1,0:T(8,128)S(1)} %copy-done), kind=kOutput, calls=%fused_computation.17 | convolution fusion | flops 6442450944 | bytes 8388608 | tf_op jit(solution)/shard_map/dot_general | solution.py:16
  114.2 1.6 copy.14
  115.8 15.0 %reduce-scatter.2.cloned.1.call-done = f32[128,512]{1,0:T(8,128)} async-done(((f32[512,512]{1,0:T(8,128)}), f32[128,512]{1,0:T(8,128)}) %reduce-scatter.2.cloned.1.call-update) | async-done | bytes 262160 | tf_op jit(solution)/shard_map/reduce_scatter | solution.py:36
  130.7 2.4 %fusion.1 = f32[128,512]{1,0:T(8,128)} fusion(f32[128,512]{1,0:T(8,128)} %reduce-scatter.2.cloned.1.call-done, f32[4,128,128]{1,2,0:T(8,128)S(1)} %bitcast_multiply_fusion, f32[4,128,512]{2,1,0:T(8,128)S(1)} %bitcast.51), kind=kOutput, calls=%fused_computation.6 | convolution fusion | flops 402718720 | bytes 1835008 | tf_op jit(solution)/shard_map/dab,dbp->ap/dot_general | solution.py:32
  133.1 48.7 %all-gather.5.cloned.1.call-done = f32[1024,512]{1,0:T(8,128)} async-done(((f32[128,512]{1,0:T(8,128)}), f32[1024,512]{1,0:T(8,128)}) %all-gather.5.cloned.1.call-update) | async-done | bytes 2097168 | tf_op jit(solution)/shard_map/all_gather | solution.py:20
  181.8 3.4 %convolution_bitcast_fusion = f32[128,512]{1,0:T(8,128)S(1)} fusion(f32[8,128,512]{2,1,0:T(8,128)} %bitcast.53, f32[8,128,128]{1,2,0:T(8,128)} %all-to-all-done, f32[8]{0:T(128)S(1)} %compare_convert_fusion.1, f32[1,8,128,128]{3,2,1,0:T(8,128)} %param.9), kind=kOutput, calls=%fused_computation.1 | convolution fusion | flops 805568512 | bytes 3407904 | tf_op jit(solution)/shard_map/jab,jbp->ap/dot_general | solution.py:25
  185.2 1.3 fusion
  186.6 4.4 %bitcast_add_fusion = f32[1024,512]{1,0:T(8,128)} fusion(f32[1024,512]{1,0:T(8,128)S(1)} %copy-done.2, f32[1024,512]{1,0:T(8,128)S(1)} %copy-done.1, f32[128,512]{1,0:T(8,128)S(1)} %fusion, f32[1024,128]{1,0:T(8,128)} %param.8), kind=kOutput, calls=%fused_computation | convolution fusion | flops 806354944 | bytes 7077888 | tf_op jit(solution)/shard_map/dot_general | solution.py:43
  (19 shorter events, 0.1 us)
Async XLA Ops:
  6.5 1.6 copy-start
  6.5 4.0 %copy-start.6 = (f32[1,128,128]{2,1,0:T(8,128)S(1)}, f32[1,128,128]{2,1,0:T(8,128)}, u32[]{:S(2)}) copy-start(f32[1,128,128]{2,1,0:T(8,128)} %param.10) | copy-start | bytes 196612
  6.5 79.3 %copy-start.5 = (f32[1,4,128,128]{3,2,1,0:T(8,128)S(1)}, f32[1,4,128,128]{3,2,1,0:T(8,128)}, u32[]{:S(2)}) copy-start(f32[1,4,128,128]{3,2,1,0:T(8,128)} %param.11) | copy-start | bytes 786436
  6.5 79.2 %all-reduce.2.cloned.1.call-start = ((), (), s32[]{:S(2)}) async-start(), calls=%async_computation.2 | async-start | bytes 524288 | tf_op jit(solution)/shard_map/psum | solution.py:30
  10.5 78.5 %copy-start.3 = (f32[128,512]{1,0:T(8,128)}, f32[128,512]{1,0:T(8,128)S(1)}, u32[]{:S(2)}) copy-start(f32[128,512]{1,0:T(8,128)S(1)} %fusion.10) | copy-start | bytes 786436
  11.9 102.3 %all-gather.7.cloned.1.call-start = ((), (), s32[]{:S(2)}) async-start(), calls=%async_computation.5 | async-start | bytes 1310720 | tf_op jit(solution)/shard_map/all_gather | solution.py:31
  85.8 3.9 %copy-start.4 = (f32[1,8,128,128]{3,2,1,0:T(8,128)S(1)}, f32[1,8,128,128]{3,2,1,0:T(8,128)}, u32[]{:S(2)}) copy-start(f32[1,8,128,128]{3,2,1,0:T(8,128)} %param.9) | copy-start | bytes 1572868
  85.8 44.9 %reduce-scatter.2.cloned.1.call-start = ((), (), s32[]{:S(2)}) async-start(), calls=%async_computation.3 | async-start | bytes 1310720 | tf_op jit(solution)/shard_map/reduce_scatter | solution.py:36
  89.1 92.8 %all-gather.5.cloned.1.call-start = ((), (), s32[]{:S(2)}) async-start(), calls=%async_computation.4 | async-start | bytes 2359296 | tf_op jit(solution)/shard_map/all_gather | solution.py:20
  90.6 42.5 %all-to-all-start = ((f32[8,128,128]{1,2,0:T(8,128)}), f32[8,128,128]{1,2,0:T(8,128)}, u32[]{:S(2)}, u32[]{:S(2)}) async-start(f32[8,128,128]{1,2,0:T(8,128)} %copy.9), calls=%async_computation | async-start | bytes 1048576 | tf_op jit(solution)/shard_map/all_to_all | solution.py:18
  181.8 4.7 %copy-start.1 = (f32[1024,512]{1,0:T(8,128)S(1)}, f32[1024,512]{1,0:T(8,128)}, u32[]{:S(2)}) copy-start(f32[1024,512]{1,0:T(8,128)} %fusion.9) | copy-start | bytes 6291460
  181.8 4.7 %copy-start.2 = (f32[1024,512]{1,0:T(8,128)S(1)}, f32[1024,512]{1,0:T(8,128)}, u32[]{:S(2)}) copy-start(f32[1024,512]{1,0:T(8,128)} %fusion.8) | copy-start | bytes 6291460
Sparse Core Ops, SparseCore 0:
  12.0 73.7 all-reduce.1
  87.3 16.0 all-gather.6
  105.9 24.7 reduce-scatter.1
  132.7 49.0 all-gather.4
where the time goes:
time: 198 us; the launch traced here: 197 us
  waiting for transfers between devices  138 us (70%)
  matrix products  37.3 us (19%)
  between operations  13.3 us (7%)
  starting transfers between devices  4.44 us (2%)
  local copies, waits for them, and re-layouts  4.31 us (2%)
    psum x1, waiting for transfers between devices, local(): g_whole = lax.psum(local_g, 'leaf')  73.8 us
    all_gather x1, waiting for transfers between devices, local(): piece = lax.all_gather(coef[None], 'leaf', axis=0, tiled=True)  48.7 us
    reduce_scatter x1, waiting for transfers between devices, local(): lax.psum_scatter(terms.reshape(number * rank_two, g_whole.shape[1]), 'clu...  15 us
    dot_general x1, matrix products, local(): jnp.dot(dense_leaf.T, probes, precision=HI)  9.6 us
    dot_general x1, matrix products, local(): jnp.dot(dense_leaf, probes, precision=HI)  9.59 us
    dot_general x1, matrix products, local(): return near + jnp.dot(leaf_basis, total, precision=HI)  4.38 us
    all_to_all x1, starting transfers between devices, local(): lax.all_to_all(cores, 'leaf', split_axis=0, concat_axis=0, tiled=True)  4.32 us
  transfers between devices with their start and end apart: 5, of which 3 were waited for; matrix products, arithmetic and copies ran while one was open for 14% of the time, Pallas kernels for 0%

commit v1 on v0

--- a/solution.py
+++ b/solution.py
@@ -27,7 +27,7 @@
     nclu = outer_cores.shape[0]
     bkeep = (jnp.arange(nclu, dtype=jnp.int32) != cown).astype(jnp.float32)[:, None, None]
     masked = outer_cores * bkeep
-    g_whole = lax.psum(local_g, "leaf")
+    g_whole = jnp.sum(lax.all_gather(local_g, "leaf"), axis=0)
     gathered = lax.all_gather(g_whole[None], "cluster", axis=0, tiled=True)
     front = jnp.einsum("dab,dbp->ap", masked, gathered, precision=HI)
     number = rank_two * lax.axis_size("cluster") // rank_two

time: 198 us -> 181 us (0.914)
  waiting for transfers between devices: 138 us -> 119 us
  local copies, waits for them, and re-layouts: 4.31 us -> 6.37 us
    psum x1 -> x0, waiting for transfers between devices: 73.8 us -> none  [local(): g_whole = lax.psum(local_g, 'leaf')]
    all_gather x0 -> x1, waiting for transfers between devices: none -> 52.4 us  [local(): g_whole = jnp.sum(lax.all_gather(local_g, 'leaf'), axis=0)]
    all_gather x1, waiting for transfers between devices: 48.7 us -> 24.6 us  [local(): piece = lax.all_gather(coef[None], 'leaf', axis=0, tiled=True)]
    all_gather x1, waiting for transfers between devices: 0.01 us -> 13.3 us  [local(): gathered = lax.all_gather(g_whole[None], 'cluster', axis=0, tiled=True)]
    reduce_scatter x1, waiting for transfers between devices: 15 us -> 25.6 us  [local(): lax.psum_scatter(terms.reshape(number * rank_two, g_whole.shape[1]), 'clu...]
    all_to_all x1, waiting for transfers between devices: 0.01 us -> 2.77 us  [local(): lax.all_to_all(cores, 'leaf', split_axis=0, concat_axis=0, tiled=True)]
    unnamed x15 -> x18, local copies, waits for them, and re-layouts: 1.73 us -> 3.8 us
  transfers between devices with their start and end apart: 5 -> 5, of which waited for: 3 -> 5; matrix products, arithmetic and copies ran while one was open for 14% -> 17% of each run, Pallas kernels for 0% -> 0%
where the time goes in v1:
time: 181 us; the launch traced here: 180 us
  waiting for transfers between devices  119 us (66%)
  matrix products  36.2 us (20%)
  between operations  13.3 us (7%)
  local copies, waits for them, and re-layouts  6.37 us (4%)
  starting transfers between devices  3.61 us (2%)
    all_gather x1, waiting for transfers between devices, local(): g_whole = jnp.sum(lax.all_gather(local_g, 'leaf'), axis=0)  52.4 us
    reduce_scatter x1, waiting for transfers between devices, local(): lax.psum_scatter(terms.reshape(number * rank_two, g_whole.shape[1]), 'clu...  25.6 us
    all_gather x1, waiting for transfers between devices, local(): piece = lax.all_gather(coef[None], 'leaf', axis=0, tiled=True)  24.6 us
    all_gather x1, waiting for transfers between devices, local(): gathered = lax.all_gather(g_whole[None], 'cluster', axis=0, tiled=True)  13.3 us
    dot_general x1, matrix products, local(): jnp.dot(dense_leaf, probes, precision=HI)  9.74 us
    dot_general x1, matrix products, local(): jnp.dot(dense_leaf.T, probes, precision=HI)  8.13 us
    dot_general x1, matrix products, local(): return near + jnp.dot(leaf_basis, total, precision=HI)  4.89 us
    unnamed x18, local copies, waits for them, and re-layouts  3.8 us
  transfers between devices with their start and end apart: 5, of which 5 were waited for; matrix products, arithmetic and copies ran while one was open for 17% of the time, Pallas kernels for 0%

profile of v1, /device:TPU:0, one launch (start us, length us, event | category | flops | bytes accessed | tf_op | source)
XLA Modules:
  0.0 180.3 jit_solution(5109149889135204773)
XLA Ops:
  6.5 1.6 copy-done
  8.1 2.4 %fusion.10 = f32[128,512]{1,0:T(8,128)S(1)} fusion(f32[1024,128]{1,0:T(8,128)} %param.8, f32[1024,512]{1,0:T(8,128)S(1)} %copy-done), kind=kOutput, calls=%fused_computation.19 | convolution fusion | flops 805306368 | bytes 2883584 | tf_op jit(solution)/shard_map/dot_general | solution.py:17
  10.6 1.3 convolution_bitcast_fusion.3
  11.9 0.7 all-gather.7.cloned.1.call-update
  12.7 52.4 %all-gather.9.cloned.1.call-done = f32[1024,512]{0,1:T(8,128)} async-done(((f32[128,512]{0,1:T(8,128)}), f32[1024,512]{0,1:T(8,128)}) %all-gather.9.cloned.1.call-update) | async-done | bytes 2097168 | tf_op jit(solution)/shard_map/all_gather | solution.py:30
  65.1 2.1 %copy.21 = f32[64,8,8,128]{3,2,1,0:T(8,128)S(1)} copy(f32[64,8,8,128]{3,1,2,0:T(8,128)} %bitcast.59) | data formatting | bytes 4194304
  67.2 1.2 bitcast_reduce_fusion
  68.4 0.0 reduce-scatter.2.cloned.1.call-start
  68.5 0.1 copy.13
  68.6 0.1 bitcast_multiply_fusion
  68.7 2.9 %fusion.11 = f32[512,512]{1,0:T(8,128)} fusion(f32[512,128]{1,0:T(8,128)S(1)} %bitcast.57, f32[128,512]{0,1:T(8,128)} %bitcast_reduce_fusion), kind=kOutput, calls=%fused_computation.20 | convolution fusion | flops 402653184 | bytes 1572864 | tf_op jit(solution)/shard_map/dba,bp->dap/dot_general | solution.py:35
  71.7 1.0 copy.12
  72.7 3.5 %all-to-all-start = ((f32[8,128,128]{1,2,0:T(8,128)}), f32[8,128,128]{1,2,0:T(8,128)S(1)}, u32[]{:S(2)}, u32[]{:S(2)}) async-start(f32[8,128,128]{1,2,0:T(8,128)} %copy.12), calls=%async_computation | async-start | bytes 1048576 | tf_op jit(solution)/shard_map/all_to_all | solution.py:18
  76.3 9.7 %fusion.8 = f32[1024,512]{1,0:T(8,128)} fusion(f32[1024,1024]{1,0:T(8,128)} %param.7, f32[1024,512]{1,0:T(8,128)S(1)} %copy-done), kind=kOutput, calls=%fused_computation.17 | convolution fusion | flops 6442450944 | bytes 8388608 | tf_op jit(solution)/shard_map/dot_general | solution.py:16
  86.0 8.1 %fusion.9 = f32[1024,512]{1,0:T(8,128)} fusion(f32[1024,1024]{1,0:T(8,128)S(1)} %copy-done.1, f32[1024,512]{1,0:T(8,128)S(1)} %copy-done), kind=kOutput, calls=%fused_computation.18 | convolution fusion | flops 6442450944 | bytes 8388608 | tf_op jit(solution)/shard_map/dot_general | solution.py:16
  94.1 2.8 %all-to-all-done = f32[8,128,128]{1,2,0:T(8,128)S(1)} async-done(((f32[8,128,128]{1,2,0:T(8,128)}), f32[8,128,128]{1,2,0:T(8,128)S(1)}, u32[]{:S(2)}, u32[]{:S(2)}) %all-to-all-start) | async-done | bytes 524320 | tf_op jit(solution)/shard_map/all_to_all | solution.py:18
  96.9 24.6 %all-gather.7.cloned.1.call-done = f32[1024,512]{1,0:T(8,128)} async-done(((f32[128,512]{1,0:T(8,128)}), f32[1024,512]{1,0:T(8,128)}) %all-gather.7.cloned.1.call-update) | async-done | bytes 2097168 | tf_op jit(solution)/shard_map/all_gather | solution.py:20
  121.4 3.6 %convolution_bitcast_fusion = f32[128,512]{1,0:T(8,128)} fusion(f32[8,128,512]{2,1,0:T(8,128)} %bitcast.58, f32[8,128,128]{1,2,0:T(8,128)S(1)} %all-to-all-done, f32[8]{0:T(128)S(1)} %compare_convert_fusion.1, f32[1,8,128,128]{3,2,1,0:T(8,128)S(1)} %copy-done.5), kind=kOutput, calls=%fused_computation.2 | convolution fusion | flops 805568512 | bytes 3407904 | tf_op jit(solution)/shard_map/jab,jbp->ap/dot_general | solution.py:25
  125.1 13.3 %all-gather.11.cloned.1.call-done = f32[512,512]{0,1:T(8,128)} async-done(((f32[128,512]{0,1:T(8,128)}), f32[512,512]{0,1:T(8,128)}) %all-gather.11.cloned.1.call-update) | async-done | bytes 1048592 | tf_op jit(solution)/shard_map/all_gather | solution.py:31
  138.4 1.6 copy.14
  139.9 25.6 %reduce-scatter.2.cloned.1.call-done = f32[128,512]{1,0:T(8,128)} async-done(((f32[512,512]{1,0:T(8,128)}), f32[128,512]{1,0:T(8,128)}) %reduce-scatter.2.cloned.1.call-update) | async-done | bytes 262160 | tf_op jit(solution)/shard_map/reduce_scatter | solution.py:36
  165.6 1.9 %fusion.1 = f32[128,512]{1,0:T(8,128)S(1)} fusion(f32[128,512]{1,0:T(8,128)} %reduce-scatter.2.cloned.1.call-done, f32[4,128,128]{1,2,0:T(8,128)S(1)} %bitcast_multiply_fusion, f32[4,128,512]{2,1,0:T(8,128)S(1)} %bitcast.56), kind=kOutput, calls=%fused_computation.7 | convolution fusion | flops 402718720 | bytes 1835008 | tf_op jit(solution)/shard_map/dab,dbp->ap/dot_general | solution.py:32
  167.5 1.3 fusion
  168.8 4.9 %bitcast_add_fusion = f32[1024,512]{1,0:T(8,128)} fusion(f32[1024,512]{1,0:T(8,128)} %fusion.8, f32[1024,512]{1,0:T(8,128)S(1)} %copy-done.2, f32[128,512]{1,0:T(8,128)S(1)} %fusion, f32[1024,128]{1,0:T(8,128)S(1)} %copy-done.4), kind=kOutput, calls=%fused_computation.1 | convolution fusion | flops 806354944 | bytes 7077888 | tf_op jit(solution)/shard_map/dot_general | solution.py:43
  (23 shorter events, 0.2 us)
Async XLA Ops:
  6.5 1.6 copy-start
  6.5 4.0 %copy-start.7 = (f32[1,128,128]{2,1,0:T(8,128)S(1)}, f32[1,128,128]{2,1,0:T(8,128)}, u32[]{:S(2)}) copy-start(f32[1,128,128]{2,1,0:T(8,128)} %param.10) | copy-start | bytes 196612
  6.5 58.6 %all-gather.9.cloned.1.call-start = ((), (), s32[]{:S(2)}) async-start(), calls=%async_computation.4 | async-start | bytes 2359296 | tf_op jit(solution)/shard_map/all_gather | solution.py:30
  10.5 1.4 copy-start.3
  11.9 109.6 %all-gather.7.cloned.1.call-start = ((), (), s32[]{:S(2)}) async-start(), calls=%async_computation.3 | async-start | bytes 2359296 | tf_op jit(solution)/shard_map/all_gather | solution.py:20
  12.6 125.7 %all-gather.11.cloned.1.call-start = ((), (), s32[]{:S(2)}) async-start(), calls=%async_computation.5 | async-start | bytes 1310720 | tf_op jit(solution)/shard_map/all_gather | solution.py:31
  67.2 1.3 copy-start.6
  68.4 3.3 %copy-start.5 = (f32[1,8,128,128]{3,2,1,0:T(8,128)S(1)}, f32[1,8,128,128]{3,2,1,0:T(8,128)}, u32[]{:S(2)}) copy-start(f32[1,8,128,128]{3,2,1,0:T(8,128)} %param.9) | copy-start | bytes 1572868
  68.4 97.2 %reduce-scatter.2.cloned.1.call-start = ((), (), s32[]{:S(2)}) async-start(), calls=%async_computation.2 | async-start | bytes 1310720 | tf_op jit(solution)/shard_map/reduce_scatter | solution.py:36
  72.7 24.2 %all-to-all-start = ((f32[8,128,128]{1,2,0:T(8,128)}), f32[8,128,128]{1,2,0:T(8,128)S(1)}, u32[]{:S(2)}, u32[]{:S(2)}) async-start(f32[8,128,128]{1,2,0:T(8,128)} %copy.12), calls=%async_computation | async-start | bytes 1048576 | tf_op jit(solution)/shard_map/all_to_all | solution.py:18
  76.2 9.8 %copy-start.1 = (f32[1024,1024]{1,0:T(8,128)S(1)}, f32[1024,1024]{1,0:T(8,128)}, u32[]{:S(2)}) copy-start(f32[1024,1024]{1,0:T(8,128)} %param.7) | copy-start | bytes 12582916
  165.6 3.2 %copy-start.2 = (f32[1024,512]{1,0:T(8,128)S(1)}, f32[1024,512]{1,0:T(8,128)}, u32[]{:S(2)}) copy-start(f32[1024,512]{1,0:T(8,128)} %fusion.9) | copy-start | bytes 6291460
  165.6 3.2 %copy-start.4 = (f32[1024,128]{1,0:T(8,128)S(1)}, f32[1024,128]{1,0:T(8,128)}, u32[]{:S(2)}) copy-start(f32[1024,128]{1,0:T(8,128)} %param.8) | copy-start | bytes 1572868
Sparse Core Ops, SparseCore 0:
  12.0 53.0 all-gather.8
  67.2 54.1 all-gather.6
  123.0 15.3 all-gather.10
  140.8 24.7 reduce-scatter.1
